TPU v7x, 256 devices: a 8x8x2 block of a 8x8x16 slice. The times are simulated.
256 devices in a mesh: grp: 2 (over z), tm: 128 (over x, y, core).
Axes of the slice: x: 8, y: 8, z: 2, core: 2. Of those that a mesh axis runs over, the one named last changes fastest.
The devices are a block of a 8x8x16 slice.
Arguments:
- samples: bfloat16 [16, 16777216], P('grp', 'tm'), parts along dimension 0, may hold values from -128 to 127, as said below
- filter_taps: bfloat16 [16, 8192], replicated, may hold values from -4 to 4
Outputs:
- channelized: bfloat16 [16, 2, 4096, 2048], P('grp', None, 'tm'), parts along dimension 0
There are 2 independent parts, one for each index of `grp`. A program takes and returns all parts, laid end to end along the dimension named above; an argument that names none is the same for every part. Nothing has to cross between parts.
Inputs may be any that keep to these rules, and one draw needn't show every extreme that they name: `samples`: every sample is a whole number, as from an 8-bit converter.
All inputs are finite; a program needn't handle non-finite values.
Results may differ from a plain program's by a relative error of at most 0.007.
Values may be sent and summed in bfloat16 or wider, within the bound.
A program may use at most 128 MiB of HBM per device.

v0:
```python
import functools
import math

import jax
import jax.numpy as jnp
import numpy as np
from jax import lax
from jax.experimental import pallas as pl
from jax.experimental.pallas import tpu as pltpu
from jax.sharding import PartitionSpec as P

MESH = pl.DeviceIdType.MESH
LANES = 128
PITCH = 136

target_level = 0.378
epsilon = 1e-06


def constants(streams, rows, half):
    t = np.arange(rows)
    lane = np.arange(LANES)
    k1 = np.arange(rows)
    k2 = np.arange(half)
    size = rows * LANES
    groups = streams // 4
    angle = 2.0 * np.pi * ((k1[:, None] * t[None, :]) % rows) / rows
    lower = rows // 2
    tables = [np.cos(angle)[:lower], np.sin(angle)[:lower]]
    tables[1][0] = np.cos(angle)[lower]
    first = np.zeros((2, groups, 4, lower, rows, streams), np.float32)
    for part, table in enumerate(tables):
        for s in range(streams):
            first[part, s // 4, s % 4, :, :, s] = table
    first = first.reshape(2 * groups * 4 * lower, rows * streams)
    upper = (rows - np.arange(lower)) % rows
    upper[0] = lower
    theta = np.stack([np.arange(lower), upper])
    theta = 2.0 * np.pi * ((theta[:, :, None] * lane) % size) / size
    twiddle = np.stack([np.cos(theta), np.sin(theta)]).astype(np.float32)
    turn = np.zeros((2, 4, lower, 4, lower), np.float32)
    for s in range(4):
        for k in range(lower):
            turn[0, s, k, s, k] = 1.0
            turn[1, s, k, s, (lower - k) % lower] = 1.0
    turn = turn.reshape(2, LANES, LANES)
    angle = 2.0 * np.pi * ((k2[:, None] * lane[None, :]) % LANES) / LANES
    cosine, sine = np.cos(angle), np.sin(angle)
    second = np.concatenate(
        [
            np.concatenate([cosine, -sine], axis=1),
            np.concatenate([-sine, -cosine], axis=1),
        ],
        axis=0,
    )
    return first, twiddle, second, turn


def kernel(
    dims,
    x_ref,
    taps_ref,
    first_ref,
    tw_ref,
    second_ref,
    recv,
    gain_ref,
    ext,
    taps_in,
    taps_wide,
    first,
    tw,
    second,
    filt,
    mixed,
    spread,
    send,
    acc,
    power_out,
    power_in,
    power_mid,
    power_cols,
    load_sem,
    halo_send_next,
    halo_send_prev,
    halo_prev,
    halo_next,
    data_send,
    data_recv,
    power_send,
    power_recv,
    power_send_mid,
    power_recv_mid,
    first_sem,
    edge_sem,
    chain_sem,
    ends_sem,
    all_sem,
):
    n, side, frames, taps, fft_len, streams, rows, half = dims
    me = lax.axis_index("tm")
    mx, my, mc = me // (2 * side), lax.rem(me // 2, side), lax.rem(me, 2)
    nxt, prv = lax.rem(me + 1, n), lax.rem(me + n - 1, n)
    width = 2 * side
    block = frames // 2
    back = taps - 1 - block

    def signal(sem, to):
        pl.semaphore_signal(sem, inc=1, device_id={"tm": to}, device_id_type=MESH)

    place = lax.rem(me, width)
    starts, ends = place == 0, place == width - 1
    barrier = pltpu.get_barrier_semaphore()

    @pl.when((me != 0) & (place < width - 1))
    def _():
        signal(barrier, nxt)

    @pl.when(me != 0)
    def _():
        signal(barrier, prv)

    @pl.when(ends)
    def _():
        for i in range(1, side):
            signal(barrier, lax.rem(me + width * i, n))

    @pl.when(me == n - 1)
    def _():
        signal(barrier, 0)

    loads = [
        pltpu.make_async_copy(taps_ref, taps_in, load_sem.at[0]),
        pltpu.make_async_copy(first_ref, first, load_sem.at[1]),
        pltpu.make_async_copy(tw_ref, tw, load_sem.at[2]),
        pltpu.make_async_copy(second_ref, second, load_sem.at[3]),
    ]
    for copy in loads:
        copy.start()
    own = []
    for f in range(frames):
        copy = pltpu.make_async_copy(
            x_ref.at[:, pl.ds(f * fft_len, fft_len)], ext.at[back + f], load_sem.at[5 + f]
        )
        copy.start()
        own.append(copy)

    expected = jnp.where(ends, side + 1, jnp.where(starts, 1, 2))
    expected = expected + jnp.where(me == 0, 1, 0)
    expected = expected - jnp.where((me == 1) | (me == n - 1), 1, 0)
    pl.semaphore_wait(barrier, expected)

    def to_next():
        for i in range(back - 1, -1, -1):
            pltpu.make_async_remote_copy(
                src_ref=x_ref.at[:, pl.ds((frames - back + i) * fft_len, fft_len)],
                dst_ref=ext.at[i],
                send_sem=halo_send_next,
                recv_sem=halo_prev,
                device_id={"tm": nxt},
                device_id_type=MESH,
            ).start()

    def to_previous():
        for i in range(block):
            pltpu.make_async_remote_copy(
                src_ref=x_ref.at[:, pl.ds(i * fft_len, fft_len)],
                dst_ref=ext.at[back + frames + i],
                send_sem=halo_send_prev,
                recv_sem=halo_next,
                device_id={"tm": prv},
                device_id_type=MESH,
            ).start()

    pl.when(me != n - 1)(to_next)
    pl.when((me == 0) | (place > 1) | ((place == 1) & (me != 1)))(to_previous)

    @pl.when(me == 0)
    def _():
        signal(first_sem, 1)
        signal(first_sem, n - 1)

    @pl.when(ends & (me != n - 1))
    def _():
        signal(edge_sem, nxt)

    @pl.when((place > 0) & (me != 1))
    def _():
        pl.semaphore_wait(chain_sem, 1)

    @pl.when((me != 0) & (place < width - 1))
    def _():
        signal(chain_sem, nxt)

    loads[0].wait()

    def widen(t, carry):
        lanes = pl.ds(pl.multiple_of(t * LANES, LANES), LANES)
        part = taps_in[:, lanes].astype(jnp.float32)
        for p in range(taps):
            taps_wide[t, p] = jnp.broadcast_to(part[p : p + 1, :], (streams, LANES))
        return carry

    lax.fori_loop(0, rows, widen, 0)

    for copy in loads[1:] + own:
        copy.wait()
    acc[...] = jnp.zeros_like(acc)

    def blanked(start, count):
        def blank(i, carry):
            ext[start + i] = jnp.zeros((streams, fft_len), jnp.bfloat16)
            return carry

        lax.fori_loop(0, count, blank, 0)

    def which_of(step):
        return lax.rem(1 + step + mc + jnp.where(me < 2, 1, 0), 2)

    def slot_of(which):
        into = lax.rem(2 * me + 1 + which, 2 * n)
        return pl.ds(pl.multiple_of(into * block, block), block)

    def send_data(step, which, to):
        pltpu.make_async_remote_copy(
            src_ref=send.at[step, to],
            dst_ref=recv.at[:, slot_of(which), :],
            send_sem=data_send,
            recv_sem=data_recv,
            device_id={"tm": to},
            device_id_type=MESH,
        ).start()

    def group(step, carry):
        which = which_of(step)
        base = which * block

        @pl.when((which == 0) & (me != 0))
        def _():
            ahead = ext.at[pl.ds(0, back)]
            pltpu.make_async_copy(ahead, ahead, halo_prev).wait()

        @pl.when((which == 0) & (me == 0))
        def _():
            blanked(0, back)

        @pl.when(which == 1)
        def _():
            behind = ext.at[pl.ds(back + frames, block)]
            pltpu.make_async_copy(behind, behind, halo_next).wait()

        @pl.when((which == 1) & (me == n - 1))
        def _():
            blanked(block, back + frames - block)

        def filtering(pair, carry):
            pieces = []
            for u in range(2):
                t = 2 * pair + u
                lanes = pl.ds(pl.multiple_of(t * LANES, LANES), LANES)
                window = [
                    ext[base + i, :, lanes].astype(jnp.float32) for i in range(taps - 1 + block)
                ]
                sums = [None] * block
                for p in range(taps):
                    weight = taps_wide[t, p]
                    for o in range(block):
                        term = weight * window[taps - 1 + o - p]
                        sums[o] = term if sums[o] is None else sums[o] + term
                pieces.append(sums)
            to = pl.ds(pl.multiple_of(pair * 2 * streams, 2 * streams), 2 * streams)
            for o in range(block):
                filt[o, to, :] = jnp.concatenate([pieces[0][o], pieces[1][o]], axis=0).astype(
                    jnp.bfloat16
                )
            return carry

        lax.fori_loop(0, rows // 2, filtering, 0)

        @pl.when((step == 0) & ends)
        def _():
            for i in range(1, side):
                signal(ends_sem, lax.rem(me + width * i, n))

        part_rows = first.shape[0] // 2
        lower = rows // 2
        tables = [[tw[part, h][None] for h in range(2)] for part in range(2)]
        top = lax.broadcasted_iota(jnp.int32, (4, 8, LANES), 1) == 0

        def first_stage(pair):
            both = jnp.concatenate([filt[2 * pair], filt[2 * pair + 1]], axis=1)
            mixed[pair % 2] = jnp.dot(first[...], both, preferred_element_type=jnp.float32)

        first_stage(0)
        for pair in range(block // 2):
            if pair + 1 < block // 2:
                first_stage(pair + 1)
            for u in range(2):
                at = pl.ds((2 * pair + u) * PITCH, 2 * half)
                lanes = slice(u * LANES, (u + 1) * LANES)
                for q in range(streams // 4):
                    rows_q = slice(q * 4 * lower, (q + 1) * 4 * lower)
                    rows_s = slice(part_rows + q * 4 * lower, part_rows + (q + 1) * 4 * lower)
                    even = mixed[pair % 2, rows_q, lanes].reshape(4, lower, LANES)
                    odd = mixed[pair % 2, rows_s, lanes].reshape(4, lower, LANES)
                    im = jnp.concatenate([jnp.where(top, 0.0, odd[:, :8]), odd[:, 8:]], axis=1)
                    re = jnp.concatenate(
                        [jnp.where(top, odd[:, :8], even[:, :8]), even[:, 8:]], axis=1
                    )
                    (cos_0, cos_1), (sin_0, sin_1) = tables
                    real = jnp.concatenate(
                        [even * cos_0 - im * sin_0, re * cos_1 + im * sin_1], axis=0
                    )
                    imag = jnp.concatenate(
                        [even * sin_0 + im * cos_0, re * sin_1 - im * cos_1], axis=0
                    )
                    twisted = jnp.concatenate(
                        [
                            real.reshape(8 * lower, LANES).astype(jnp.bfloat16),
                            imag.reshape(8 * lower, LANES).astype(jnp.bfloat16),
                        ],
                        axis=1,
                    )
                    spec = lax.dot_general(
                        second[...],
                        twisted,
                        (((1,), (1,)), ((), ())),
                        preferred_element_type=jnp.float32,
                    )
                    spread[2 * q, at, :] = spec[:, :LANES]
                    spread[2 * q + 1, at, :] = spec[:, LANES:]

        def packing(k, carry):
            sums = list(carry)
            for h in range(2):
                for q in range(streams // 4):
                    for part in range(2):
                        piece = spread.at[2 * q + h][pl.ds(part * half + k, block, stride=PITCH), :]
                        piece = piece.astype(jnp.bfloat16)
                        send[step, 2 * k + h, 2 * q + part] = piece
                        wide = piece.astype(jnp.float32)
                        sums[q] = sums[q] + wide * wide
            return tuple(sums)

        sums = lax.fori_loop(
            0, half, packing, tuple(acc[q] for q in range(streams // 4)), unroll=2
        )
        for q in range(streams // 4):
            acc[q] = sums[q]

        @pl.when((step == 0) & starts & (me != 0))
        def _():
            pl.semaphore_wait(edge_sem, 1)
            to_previous()

        @pl.when((step == 0) & (me == 1))
        def _():
            pl.semaphore_wait(first_sem, 1)
            to_previous()

        @pl.when((step == 0) & ends)
        def _():
            pl.semaphore_wait(ends_sem, side - 1)
            for i in range(1, width):
                to = me - i

                @pl.when(to != 0)
                def _():
                    signal(all_sem, to)

        @pl.when((step == 0) & jnp.logical_not(ends))
        def _():
            pl.semaphore_wait(all_sem, 1)

        @pl.when((step == 0) & (me == 1))
        def _():
            signal(all_sem, 0)

        @pl.when((step == 0) & (me == 0))
        def _():
            def here(i, carry):
                signal(first_sem, i)
                return carry

            lax.fori_loop(2, n - 1, here, 0, unroll=4)

        @pl.when((step == 1) & (me > 1))
        def _():
            pl.semaphore_wait(first_sem, 1)

        @pl.when(step == 1)
        def _():
            lane = lax.broadcasted_iota(jnp.int32, (block, LANES), 1)
            low = acc[0] + pltpu.roll(acc[0], LANES - 16, 1)
            high = acc[1] + pltpu.roll(acc[1], LANES - 16, 1)
            row = jnp.where(lane % 32 < 16, low, pltpu.roll(high, 16, 1))
            row = jnp.sum(row, axis=0, keepdims=True)
            power_out[...] = row
            power_in[place] = row
            for i in range(1, width):
                to = lax.rem(place + i, width)
                pltpu.make_async_remote_copy(
                    src_ref=power_out,
                    dst_ref=power_in.at[place],
                    send_sem=power_send,
                    recv_sem=power_recv,
                    device_id={"tm": mx * width + to},
                    device_id_type=MESH,
                ).start()

        def sending(d, carry):
            pair = d // 2
            dy = lax.rem(pair, side)
            dx = lax.rem(pair // side + 3 * dy, side)
            to = (
                lax.rem(mx + dx, side) * width
                + lax.rem(my + dy, side) * 2
                + lax.rem(mc + lax.rem(d, 2), 2)
            )

            @pl.when((to != 0) | (step == 1) | (me == 0))
            def _():
                send_data(step, which, to)

            @pl.when((to == 0) & (step == 1))
            def _():
                send_data(0, which_of(0), to)

            return carry

        lax.fori_loop(1, n, sending, 0, unroll=4)
        return carry

    lax.fori_loop(0, 2, group, 0)

    kept = []
    for step in range(2):
        copy = pltpu.make_async_copy(
            send.at[step, me], recv.at[:, slot_of(which_of(step)), :], load_sem.at[3 + step]
        )
        copy.start()
        kept.append(copy)

    others = power_in.at[pl.ds(0, width - 1)]
    pltpu.make_async_copy(others, others, power_recv).wait()
    row = jnp.sum(power_in[...], axis=0)
    power_mid[...] = row
    power_cols[mx] = row
    for i in range(1, side):
        pltpu.make_async_remote_copy(
            src_ref=power_mid,
            dst_ref=power_cols.at[mx],
            send_sem=power_send_mid,
            recv_sem=power_recv_mid,
            device_id={"tm": lax.rem(me + width * i, n)},
            device_id_type=MESH,
        ).start()
    columns = power_cols.at[pl.ds(0, side - 1)]
    pltpu.make_async_copy(columns, columns, power_recv_mid).wait()
    total = jnp.sum(power_cols[...], axis=0)
    lane = lax.broadcasted_iota(jnp.int32, (1, LANES), 1)
    count = frames * n * half * rows
    gains = []
    for s in range(streams):
        start = (s % 4) * 32 + (s // 4) * 16
        power = jnp.sum(
            jnp.where((lane >= start) & (lane < start + 16), total, 0.0), axis=1, keepdims=True
        )
        gains.append(target_level / jnp.sqrt(power / count + epsilon))

    level = jnp.zeros((streams, LANES), jnp.float32)
    index = lax.broadcasted_iota(jnp.int32, (streams, LANES), 0)
    for s in range(streams):
        level = jnp.where(index == s, gains[s], level)
    gain_ref[...] = level

    arrived = recv.at[:, pl.ds(0, (n - 1) * frames), :]
    pltpu.make_async_copy(arrived, arrived, data_recv).wait()
    for copy in kept:
        copy.wait()

    @pl.when(me != n - 1)
    def _():
        sent = ext.at[pl.ds(0, back)]
        pltpu.make_async_copy(sent, sent, halo_send_next).wait()

    sent = ext.at[pl.ds(0, block)]
    pltpu.make_async_copy(sent, sent, halo_send_prev).wait()
    pltpu.make_async_copy(arrived, arrived, data_send).wait()
    pltpu.make_async_copy(others, others, power_send).wait()
    pltpu.make_async_copy(columns, columns, power_send_mid).wait()


def finish(rows, turn_ref, gain_ref, spectra_ref, out_ref):
    for q in range(spectra_ref.shape[0] // 2):
        for part in range(2):
            turned = lax.dot_general(
                turn_ref[...],
                spectra_ref[2 * q + part],
                (((1,), (1,)), ((), ())),
                preferred_element_type=jnp.float32,
            )
            for s in range(4):
                gain = gain_ref[4 * q + s : 4 * q + s + 1, :1]
                scaled = turned[s * rows : (s + 1) * rows, :] * gain
                out_ref[4 * q + s, part] = jnp.clip(scaled, -1.0, 1.0).astype(jnp.bfloat16)


def solution(mesh):
    n = mesh.shape["tm"]
    side = math.isqrt(n // 2)

    def on_device(samples, filter_taps):
        streams, length = samples.shape
        taps, fft_len = filter_taps.shape
        frames = length // fft_len
        rows = fft_len // LANES
        half = rows
        block = frames // 2
        back = taps - 1 - block
        first, twiddle, second, turn = constants(streams, rows, half)
        first = jnp.asarray(first, jnp.bfloat16)
        second = jnp.asarray(second, jnp.bfloat16)
        eye = jnp.asarray(turn, jnp.bfloat16)
        dims = (n, side, frames, taps, fft_len, streams, rows, half)
        tiles = streams // 4
        per = fft_len // 2 // n

        def body(*refs):
            kernel(dims, *refs)

        anywhere = pl.BlockSpec(memory_space=pltpu.HBM)
        dma = pltpu.SemaphoreType.DMA
        spectra, gain = pl.pallas_call(
            body,
            out_shape=(
                jax.ShapeDtypeStruct((2 * tiles, n * frames, LANES), jnp.bfloat16),
                jax.ShapeDtypeStruct((streams, LANES), jnp.float32),
            ),
            in_specs=[anywhere] * 5,
            out_specs=(anywhere, pl.BlockSpec(memory_space=pltpu.VMEM)),
            scratch_shapes=[
                pltpu.VMEM((back + frames + block, streams, fft_len), jnp.bfloat16),
                pltpu.VMEM((taps, fft_len), jnp.bfloat16),
                pltpu.VMEM((rows, taps, streams, LANES), jnp.float32),
                pltpu.VMEM(first.shape, jnp.bfloat16),
                pltpu.VMEM(twiddle.shape, jnp.float32),
                pltpu.VMEM(second.shape, jnp.bfloat16),
                pltpu.VMEM((block, rows * streams, LANES), jnp.bfloat16),
                pltpu.VMEM((2, first.shape[0], 2 * LANES), jnp.float32),
                pltpu.VMEM((2 * tiles, block * PITCH, LANES), jnp.float32),
                pltpu.VMEM((2, n, 2 * tiles, block, LANES), jnp.bfloat16),
                pltpu.VMEM((tiles, block, LANES), jnp.float32),
                pltpu.VMEM((1, LANES), jnp.float32),
                pltpu.VMEM((2 * side, 1, LANES), jnp.float32),
                pltpu.VMEM((1, LANES), jnp.float32),
                pltpu.VMEM((side, 1, LANES), jnp.float32),
                dma((5 + frames,)),
                dma,
                dma,
                dma,
                dma,
                dma,
                dma,
                dma,
                dma,
                dma,
                dma,
                pltpu.SemaphoreType.REGULAR,
                pltpu.SemaphoreType.REGULAR,
                pltpu.SemaphoreType.REGULAR,
                pltpu.SemaphoreType.REGULAR,
                pltpu.SemaphoreType.REGULAR,
            ],
            compiler_params=pltpu.CompilerParams(
                collective_id=1, has_side_effects=True, vmem_limit_bytes=63 * 1024 * 1024
            ),
        )(samples, filter_taps, first, jnp.asarray(twiddle), second)

        cols = 1024

        def by_half(i):
            return (lax.rem(lax.axis_index("tm"), 2), 0, 0)

        return pl.pallas_call(
            functools.partial(finish, rows // 2),
            grid=(frames * n // cols,),
            out_shape=jax.ShapeDtypeStruct((streams, 2, per, frames * n), jnp.bfloat16),
            in_specs=[
                pl.BlockSpec((None, LANES, LANES), by_half),
                pl.BlockSpec((streams, LANES), lambda i: (0, 0)),
                pl.BlockSpec((2 * tiles, cols, LANES), lambda i: (0, i, 0)),
            ],
            out_specs=pl.BlockSpec((streams, 2, per, cols), lambda i: (0, 0, 0, i)),
        )(eye, gain, spectra)

    return jax.shard_map(
        on_device,
        mesh=mesh,
        in_specs=(P("grp", "tm"), P()),
        out_specs=P("grp", None, "tm", None),
        check_vma=False,
    )
```

profile of v0, /device:TPU:513, one launch (start us, length us, event | category | flops | bytes accessed | tf_op | source)
XLA Modules:
  0.0 84.3 jit_solution(8189742086946343980)
XLA Ops:
  0.0 81.0 %shard_map.64 = (bf16[4,2048,128]{2,1,0:T(8,128)(2,1)}, f32[8,128]{1,0:T(8,128)}) custom-call(bf16[8,131072]{1,0:T(8,128)(2,1)} %refs_0_.1, bf16[16,8192]{1,0:T(8,128)(2,1)} %refs_1_.1, bf16[512,512]{1,0:T(8,128)(2,1)} %constant.8.clone.refs_2_, f32[2,2,32,128]{3,2,1,0:T(8,128)} %constant.11.clone.refs_3_, bf16[128,256]{1,0:T(8,128)(2,1)} %constant.9.clone.refs_4_), custom_call_target="tpu_custom_call" | custom-call | tf_op jit(solution)/shard_map/pallas_call | solution.py:534
  81.1 3.2 %shard_map.65 = bf16[8,2,32,2048]{3,2,1,0:T(8,128)(2,1)} custom-call(bf16[2,128,128]{2,1,0:T(8,128)(2,1)} %constant.10.clone.turn_ref, f32[8,128]{1,0:T(8,128)} %get-tuple-element.7.gain_ref, bf16[4,2048,128]{2,1,0:T(8,128)(2,1)} %get-tuple-element.8.spectra_ref), custom_call_target="tpu_custom_call" | custom-call | tf_op jit(solution)/shard_map/pallas_call | solution.py:585
where the time goes:
time: 84.4 us; the launch traced here: 84.3 us
  Pallas kernels  84.3 us (100%)
    pallas_call x1, Pallas kernels, on_device(): pl.pallas_call(body, out_shape=(jax.ShapeDtypeStruct((2 * tiles, n * fram...  81 us
    pallas_call x1, Pallas kernels, on_device(): pl.pallas_call(functools.partial(finish, rows // 2), grid=(frames * n //...  3.23 us

commit v1 on v0

--- a/solution.py
+++ b/solution.py
@@ -219,12 +219,12 @@
 
     def slot_of(which):
         into = lax.rem(2 * me + 1 + which, 2 * n)
-        return pl.ds(pl.multiple_of(into * block, block), block)
+        return into
 
     def send_data(step, which, to):
         pltpu.make_async_remote_copy(
             src_ref=send.at[step, to],
-            dst_ref=recv.at[:, slot_of(which), :],
+            dst_ref=recv.at[slot_of(which)],
             send_sem=data_send,
             recv_sem=data_recv,
             device_id={"tm": to},
@@ -436,7 +436,7 @@
     kept = []
     for step in range(2):
         copy = pltpu.make_async_copy(
-            send.at[step, me], recv.at[:, slot_of(which_of(step)), :], load_sem.at[3 + step]
+            send.at[step, me], recv.at[slot_of(which_of(step))], load_sem.at[3 + step]
         )
         copy.start()
         kept.append(copy)
@@ -474,7 +474,7 @@
         level = jnp.where(index == s, gains[s], level)
     gain_ref[...] = level
 
-    arrived = recv.at[:, pl.ds(0, (n - 1) * frames), :]
+    arrived = recv.at[pl.ds(0, 2 * (n - 1))]
     pltpu.make_async_copy(arrived, arrived, data_recv).wait()
     for copy in kept:
         copy.wait()
@@ -492,11 +492,11 @@
 
 
 def finish(rows, turn_ref, gain_ref, spectra_ref, out_ref):
-    for q in range(spectra_ref.shape[0] // 2):
+    for q in range(spectra_ref.shape[1] // 2):
         for part in range(2):
             turned = lax.dot_general(
                 turn_ref[...],
-                spectra_ref[2 * q + part],
+                spectra_ref[:, 2 * q + part].reshape(-1, LANES),
                 (((1,), (1,)), ((), ())),
                 preferred_element_type=jnp.float32,
             )
@@ -534,7 +534,7 @@
         spectra, gain = pl.pallas_call(
             body,
             out_shape=(
-                jax.ShapeDtypeStruct((2 * tiles, n * frames, LANES), jnp.bfloat16),
+                jax.ShapeDtypeStruct((2 * n, 2 * tiles, block, LANES), jnp.bfloat16),
                 jax.ShapeDtypeStruct((streams, LANES), jnp.float32),
             ),
             in_specs=[anywhere] * 5,
@@ -589,7 +589,7 @@
             in_specs=[
                 pl.BlockSpec((None, LANES, LANES), by_half),
                 pl.BlockSpec((streams, LANES), lambda i: (0, 0)),
-                pl.BlockSpec((2 * tiles, cols, LANES), lambda i: (0, i, 0)),
+                pl.BlockSpec((cols // block, 2 * tiles, block, LANES), lambda i: (i, 0, 0, 0)),
             ],
             out_specs=pl.BlockSpec((streams, 2, per, cols), lambda i: (0, 0, 0, i)),
         )(eye, gain, spectra)

time: 84.4 us -> 84.4 us (level)
  no operation moved by 1% of the time
where the time goes in v1:
time: 84.4 us; the launch traced here: 84.3 us
  Pallas kernels  84.3 us (100%)
    pallas_call x1, Pallas kernels, on_device(): pl.pallas_call(body, out_shape=(jax.ShapeDtypeStruct((2 * n, 2 * tiles, b...  81.1 us
    pallas_call x1, Pallas kernels, on_device(): pl.pallas_call(functools.partial(finish, rows // 2), grid=(frames * n //...  3.18 us

profile of v1, /device:TPU:513, one launch (start us, length us, event | category | flops | bytes accessed | tf_op | source)
XLA Modules:
  0.0 84.3 jit_solution(18286064882288371308)
XLA Ops:
  0.0 81.1 %shard_map.64 = (bf16[256,4,8,128]{3,2,1,0:T(8,128)(2,1)}, f32[8,128]{1,0:T(8,128)}) custom-call(bf16[8,131072]{1,0:T(8,128)(2,1)} %refs_0_.1, bf16[16,8192]{1,0:T(8,128)(2,1)} %refs_1_.1, bf16[512,512]{1,0:T(8,128)(2,1)} %constant.8.clone.refs_2_, f32[2,2,32,128]{3,2,1,0:T(8,128)} %constant.11.clone.refs_3_, bf16[128,256]{1,0:T(8,128)(2,1)} %constant.9.clone.refs_4_), custom_call_target="tpu_custom_call" | custom-call | tf_op jit(solution)/shard_map/pallas_call | solution.py:534
  81.1 3.2 %shard_map.65 = bf16[8,2,32,2048]{3,2,1,0:T(8,128)(2,1)} custom-call(bf16[2,128,128]{2,1,0:T(8,128)(2,1)} %constant.10.clone.turn_ref, f32[8,128]{1,0:T(8,128)} %get-tuple-element.7.gain_ref, bf16[256,4,8,128]{3,2,1,0:T(8,128)(2,1)} %get-tuple-element.8.spectra_ref), custom_call_target="tpu_custom_call" | custom-call | tf_op jit(solution)/shard_map/pallas_call | solution.py:585
